TPU v7x, 32 devices: a whole 2x2x4 slice. The times are simulated.
32 devices in a mesh: sec: 4 (over y, core), grp: 8 (over z, x).
Axes of the slice: x: 2, y: 2, z: 4, core: 2. Of those that a mesh axis runs over, the one named last changes fastest.
Arguments:
- positions: float32 [3, 16384], P(None, ('sec', 'grp')), may hold values from -9 to 9, as said below
- velocities: float32 [3, 16384], P(None, ('sec', 'grp')), may hold values from -4 to 4
- masses: float32 [16384], P(('sec', 'grp')), may hold values from 0.004 to 0.04
- near_list: int32 [64, 64], P(('sec', 'grp')), may hold values from 0 to 7, as said below
- near_count: int32 [64], P(('sec', 'grp')), may hold values from 1 to 64, as said below
- far_list: int32 [64, 32], P(('sec', 'grp')), may hold values from 0 to 63
Outputs:
- positions_out: float32 [3, 16384], P(None, ('sec', 'grp'))
- velocities_out: float32 [3, 16384], P(None, ('sec', 'grp'))
- accel_out: float32 [3, 16384], P(None, ('sec', 'grp'))
Inputs may be any that keep to these rules, and one draw needn't show every extreme that they name: `positions`: within the range stated, particles of a block lie near one another and blocks of a group near their group. `near_list`: numbers within the group: the section index times 2 plus the block's place on its device. Slot 0 names the block itself. `near_count`: some block has all 64 slots used.
All inputs are finite; a program needn't handle non-finite values.
Results may differ from a plain program's by a relative error of at most 0.0001.
Values sent between devices are 32-bit elements; how exact they have to be, the bound alone decides.
A program may use at most 64 MiB of HBM per device.

v0:
```python
import functools

import jax
import jax.numpy as jnp
from jax import lax
from jax.experimental import pallas as pl
from jax.experimental.pallas import tpu as pltpu
from jax.sharding import PartitionSpec as P

timestep = 0.05
softening = 0.25
LANES = 128
ROWS = 8
MESH = pl.DeviceIdType.MESH


def peer(sec, r, n_sec):
    if n_sec % 2:
        return lax.rem(sec + r, n_sec)
    pair = lax.rem(sec // 2 + r // 2, n_sec // 2)
    return pair * 2 + lax.rem(sec + r, 2)


def own_moments(blocks):
    lane = lax.broadcasted_iota(jnp.int32, (1, LANES), 1)
    rows = []
    for x, y, z, m in blocks:
        total = lambda v: jnp.sum(v, axis=1, keepdims=True)
        mass = total(m)
        cx, cy, cz = total(m * x) / mass, total(m * y) / mass, total(m * z) / mass
        dx, dy, dz = x - cx, y - cy, z - cz
        radius = dx * dx + dy * dy + dz * dz
        numbers = (
            mass,
            cx,
            cy,
            cz,
            total(m * (3.0 * dx * dx - radius)),
            total(m * (3.0 * dy * dy - radius)),
            total(m * (3.0 * dz * dz - radius)),
            total(3.0 * m * dx * dy),
            total(3.0 * m * dx * dz),
            total(3.0 * m * dy * dz),
        )
        row = jnp.zeros((1, LANES), jnp.float32)
        for place, number in enumerate(numbers):
            row = jnp.where(lane == place, number, row)
        rows.append(row)
    return rows


def far_part(target, moment):
    number = [moment[:, k : k + 1] for k in range(10)]
    mass, cx, cy, cz, qxx, qyy, qzz, qxy, qxz, qyz = number
    rx, ry, rz = target[0] - cx, target[1] - cy, target[2] - cz
    square = rx * rx + ry * ry + rz * rz + softening
    inv = lax.rsqrt(square)
    inv_two = inv * inv
    inv_three = inv_two * inv
    inv_five = inv_three * inv_two
    quad_x = qxx * rx + qxy * ry + qxz * rz
    quad_y = qxy * rx + qyy * ry + qyz * rz
    quad_z = qxz * rx + qyz * ry + qzz * rz
    inner = rx * quad_x + ry * quad_y + rz * quad_z
    radial = 2.5 * inner * inv_two * inv_five - mass * inv_three
    total = lambda v: jnp.sum(v, axis=0, keepdims=True)
    return (
        total(radial * rx - quad_x * inv_five),
        total(radial * ry - quad_y * inv_five),
        total(radial * rz - quad_z * inv_five),
    )


def kernel(
    n_sec,
    n_grp,
    pos_hbm,
    vel_hbm,
    mass_hbm,
    near_hbm,
    count_hbm,
    far_hbm,
    half_out,
    vel_out,
    direct_out,
    far_out,
    pos_ref,
    vel_ref,
    mass_ref,
    near_ref,
    count_ref,
    far_ref,
    load_sem,
    ghosts,
    gathered,
    times,
    send_sem,
    recv_sem,
    moment_send,
    moment_recv,
):
    n_dev = n_sec * n_grp
    local_blocks = near_ref.shape[0]
    slots = near_ref.shape[1]
    particles = pos_ref.shape[1]
    block_size = particles // local_blocks
    group_blocks = n_sec * local_blocks
    all_blocks = n_dev * local_blocks
    sec = lax.axis_index("sec")
    grp = lax.axis_index("grp")
    me = sec * n_grp + grp

    loads = [
        pltpu.make_async_copy(source, target, load_sem.at[k])
        for k, (source, target) in enumerate(
            (
                (pos_hbm, pos_ref),
                (vel_hbm, vel_ref),
                (mass_hbm, mass_ref),
                (near_hbm, near_ref),
                (count_hbm, count_ref),
                (far_hbm, far_ref),
            )
        )
    ]
    for load in loads:
        load.start()
    barrier = pltpu.get_barrier_semaphore()

    def greet(r, carry):
        other = lax.rem(me + r, n_dev)
        pl.semaphore_signal(
            barrier,
            inc=1,
            device_id={"sec": other // n_grp, "grp": lax.rem(other, n_grp)},
            device_id_type=MESH,
        )
        return carry

    lax.fori_loop(1, n_dev, greet, 0)
    for load in loads:
        load.wait()

    number = lax.broadcasted_iota(jnp.int32, (group_blocks, slots), 0)
    slot = lax.broadcasted_iota(jnp.int32, (group_blocks, slots), 1)
    for b in range(local_blocks):
        used = jnp.where(
            (near_ref[b : b + 1, :] == number) & (slot < count_ref[b]), 1.0, 0.0
        )
        times[b] = jnp.broadcast_to(
            jnp.sum(used, axis=1, keepdims=True), (group_blocks, LANES)
        )
    entries = far_ref.shape[1]
    block_number = lax.broadcasted_iota(jnp.int32, (all_blocks, entries), 0)
    chosen = [
        jnp.where(far_ref[b : b + 1, :] == block_number, 1.0, 0.0)
        for b in range(local_blocks)
    ]

    current = pos_ref[...]
    speed = vel_ref[...]
    tiles = particles // LANES
    tiles_of_block = block_size // LANES
    for step in range(2):
        half = current + 0.5 * timestep * speed
        ghosts[step, sec, 0:3, :] = half
        ghosts[step, sec, 3:4, :] = mass_ref[...]
        if step == 0:
            pl.semaphore_wait(barrier, n_dev - 1)

        def send_particles(r, carry):
            other = lax.rem(sec + r, n_sec)
            pltpu.make_async_remote_copy(
                src_ref=ghosts.at[step, sec],
                dst_ref=ghosts.at[step, sec],
                send_sem=send_sem.at[step, other],
                recv_sem=recv_sem.at[step, sec],
                device_id={"sec": other, "grp": grp},
                device_id_type=MESH,
            ).start()
            return carry

        lax.fori_loop(1, n_sec, send_particles, 0)

        blocks = []
        for b in range(local_blocks):
            cut = slice(b * block_size, (b + 1) * block_size)
            blocks.append(
                (half[0:1, cut], half[1:2, cut], half[2:3, cut], mass_ref[0:1, cut])
            )
        for b, row in enumerate(own_moments(blocks)):
            gathered[step, me * local_blocks + b] = row

        def send_moments(r, carry):
            other = lax.rem(me + r, n_dev)
            mine = gathered.at[step, pl.ds(me * local_blocks, local_blocks)]
            pltpu.make_async_remote_copy(
                src_ref=mine,
                dst_ref=mine,
                send_sem=moment_send.at[step],
                recv_sem=moment_recv.at[step],
                device_id={"sec": other // n_grp, "grp": lax.rem(other, n_grp)},
                device_id_type=MESH,
            ).start()
            return carry

        lax.fori_loop(1, n_dev, send_moments, 0)

        def add_device(r, totals):
            other = peer(sec, r, n_sec)

            @pl.when(r > 0)
            def _():
                pltpu.make_async_copy(
                    ghosts.at[step, other], ghosts.at[step, other], recv_sem.at[step, other]
                ).wait()

            totals = [list(t) for t in totals]
            for tile in range(tiles):
                rows = ghosts[step, other, :, tile * LANES : (tile + 1) * LANES]
                columns = jnp.transpose(rows)
                place = tile // tiles_of_block
                weights = [
                    times[b, pl.ds(other * local_blocks + place, 1), :]
                    for b in range(local_blocks)
                ]
                for part in range(LANES // ROWS):
                    cut = slice(part * ROWS, (part + 1) * ROWS)
                    sx, sy, sz, sm = (
                        jnp.broadcast_to(columns[cut, c : c + 1], (ROWS, LANES)) for c in range(4)
                    )
                    scaled = [sm * w for w in weights]
                    for t in range(tiles):
                        lanes = slice(t * LANES, (t + 1) * LANES)
                        dx = sx - half[0:1, lanes]
                        dy = sy - half[1:2, lanes]
                        dz = sz - half[2:3, lanes]
                        inv = lax.rsqrt(dx * dx + dy * dy + (dz * dz + softening))
                        weight = scaled[t // tiles_of_block] * inv * (inv * inv)
                        totals[t][0] = totals[t][0] + weight * dx
                        totals[t][1] = totals[t][1] + weight * dy
                        totals[t][2] = totals[t][2] + weight * dz
            return tuple(tuple(t) for t in totals)

        zero = jnp.zeros((ROWS, LANES), jnp.float32)
        totals = lax.fori_loop(0, n_sec, add_device, tuple((zero,) * 3 for _ in range(tiles)))
        direct = jnp.concatenate(
            [
                jnp.concatenate(
                    [jnp.sum(totals[t][c], axis=0, keepdims=True) for t in range(tiles)], axis=1
                )
                for c in range(3)
            ],
            axis=0,
        )

        others = gathered.at[step, pl.ds(0, (n_dev - 1) * local_blocks)]
        pltpu.make_async_copy(others, others, moment_recv.at[step]).wait()
        table = gathered[step].reshape(all_blocks, LANES)
        far = []
        for b in range(local_blocks):
            moment = lax.dot_general(
                chosen[b],
                table,
                (((0,), (0,)), ((), ())),
                precision=lax.Precision.HIGHEST,
                preferred_element_type=jnp.float32,
            )
            cut = slice(b * block_size, (b + 1) * block_size)
            far.append(
                jnp.concatenate(
                    far_part((half[0:1, cut], half[1:2, cut], half[2:3, cut]), moment), axis=0
                )
            )
        far = jnp.concatenate(far, axis=1)
        if step == 0:
            speed = speed + timestep * (direct + far)
            current = half + 0.5 * timestep * speed
            vel_out[...] = speed
        else:
            half_out[...] = half
            direct_out[...] = direct
            far_out[...] = far

    for step in range(2):

        def sent(r, carry):
            other = lax.rem(sec + r, n_sec)
            pltpu.make_async_copy(
                ghosts.at[step, sec], ghosts.at[step, sec], send_sem.at[step, other]
            ).wait()
            return carry

        lax.fori_loop(1, n_sec, sent, 0)
        others = gathered.at[step, pl.ds(0, (n_dev - 1) * local_blocks)]
        pltpu.make_async_copy(others, others, moment_send.at[step]).wait()


def on_device(n_sec, n_grp, positions, velocities, masses, near_list, near_count, far_list):
    particles = positions.shape[1]
    local_blocks = near_list.shape[0]
    vmem = pl.BlockSpec(memory_space=pltpu.VMEM)
    half, speed, direct, far = pl.pallas_call(
        functools.partial(kernel, n_sec, n_grp),
        out_shape=[jax.ShapeDtypeStruct(positions.shape, jnp.float32)] * 4,
        in_specs=[pl.BlockSpec(memory_space=pltpu.HBM)] * 6,
        out_specs=[vmem] * 4,
        scratch_shapes=[
            pltpu.VMEM(positions.shape, jnp.float32),
            pltpu.VMEM(velocities.shape, jnp.float32),
            pltpu.VMEM((1, particles), jnp.float32),
            pltpu.VMEM(near_list.shape, jnp.int32),
            pltpu.SMEM(near_count.shape, jnp.int32),
            pltpu.VMEM(far_list.shape, jnp.int32),
            pltpu.SemaphoreType.DMA((6,)),
            pltpu.VMEM((2, n_sec, 4, particles), jnp.float32),
            pltpu.VMEM((2, n_sec * n_grp * local_blocks, 1, LANES), jnp.float32),
            pltpu.VMEM((local_blocks, n_sec * local_blocks, LANES), jnp.float32),
            pltpu.SemaphoreType.DMA((2, n_sec)),
            pltpu.SemaphoreType.DMA((2, n_sec)),
            pltpu.SemaphoreType.DMA((2,)),
            pltpu.SemaphoreType.DMA((2,)),
        ],
        compiler_params=pltpu.CompilerParams(
            collective_id=0, has_side_effects=True
        ),
        name="leapfrog",
    )(positions, velocities, masses[None, :], near_list, near_count, far_list)
    accel = direct + far
    speed = speed + timestep * accel
    return half + 0.5 * timestep * speed, speed, accel


def solution(mesh):
    placed = (
        P(None, ("sec", "grp")),
        P(None, ("sec", "grp")),
        P(("sec", "grp")),
        P(("sec", "grp"), None),
        P(("sec", "grp")),
        P(("sec", "grp"), None),
    )
    return jax.shard_map(
        functools.partial(on_device, mesh.shape["sec"], mesh.shape["grp"]),
        mesh=mesh,
        in_specs=placed,
        out_specs=(P(None, ("sec", "grp")), P(None, ("sec", "grp")), P(None, ("sec", "grp"))),
        check_vma=False,
    )
```

profile of v0, /device:TPU:0, one launch (start us, length us, event | category | flops | bytes accessed | tf_op | source)
XLA Modules:
  0.0 20.7 jit_solution(15445198818304787671)
XLA Ops:
  0.6 18.7 %leapfrog.1 = (f32[3,512]{1,0:T(4,128)}, f32[3,512]{1,0:T(4,128)}, f32[3,512]{1,0:T(4,128)}, f32[3,512]{1,0:T(4,128)}) custom-call(f32[3,512]{1,0:T(4,128)} %pos_hbm.1, f32[3,512]{1,0:T(4,128)} %vel_hbm.1, f32[1,512]{1,0:T(1,128)} %bitcast.1, s32[2,64]{1,0:T(2,128)} %near_hbm.1, s32[2]{0:T(128)} %count_hbm.1, s32[2,32]{1,0:T(2,128)} %far_hbm.1), custom_call_target="tpu_custom_call" | custom-call | tf_op jit(solution)/shard_map/leapfrog/pallas_call | solution.py:303
  19.3 1.4 %multiply_add_fusion = (f32[3,512]{1,0:T(4,128)}, f32[3,512]{1,0:T(4,128)}, f32[3,512]{1,0:T(4,128)}) fusion(f32[3,512]{1,0:T(4,128)} %get-tuple-element.7, f32[3,512]{1,0:T(4,128)} %get-tuple-element.8, f32[3,512]{1,0:T(4,128)} %get-tuple-element.9, f32[3,512]{1,0:T(4,128)} %get-tuple-element.10), kind=kLoop, calls=%fused_computation | loop fusion | flops 7680 | bytes 43008 | tf_op jit(solution)/shard_map/add | solution.py:331
where the time goes:
time: 20.9 us; the launch traced here: 20.7 us
  Pallas kernels  18.7 us (89%)
  other arithmetic  1.36 us (7%)
  between operations  0.64 us (3%)
    pallas_call x1, Pallas kernels, on_device(): pl.pallas_call(functools.partial(kernel, n_sec, n_grp), out_shape=[jax.Sh...  18.7 us
    add x1, other arithmetic, on_device(): return (half + 0.5 * timestep * speed, speed, accel)  1.36 us

commit v1 on v0

--- a/solution.py
+++ b/solution.py
@@ -322,10 +322,10 @@
             pltpu.SemaphoreType.DMA((2,)),
         ],
         compiler_params=pltpu.CompilerParams(
-            collective_id=0, has_side_effects=True
+            collective_id=0, has_side_effects=True, vmem_limit_bytes=16 * 1024 * 1024
         ),
         name="leapfrog",
-    )(positions, velocities, masses[None, :], near_list, near_count, far_list)
+    )(*[pltpu.with_memory_space_constraint(v, pltpu.HBM) for v in (positions, velocities, masses[None, :], near_list, near_count, far_list)])
     accel = direct + far
     speed = speed + timestep * accel
     return half + 0.5 * timestep * speed, speed, accel

time: 20.9 us -> 19.5 us (0.933)
  other arithmetic: 1.36 us -> 0.61 us
  Pallas kernels: 18.7 us -> 18.1 us
    add x1, other arithmetic: 1.36 us -> 0.61 us  [on_device(): return (half + 0.5 * timestep * speed, speed, accel)]
    pallas_call x1, Pallas kernels: 18.7 us -> 18.1 us  [on_device(): pl.pallas_call(functools.partial(kernel, n_sec, n_grp), out_shape=[jax.Sh...]
where the time goes in v1:
time: 19.5 us; the launch traced here: 19.3 us
  Pallas kernels  18.1 us (93%)
  between operations  0.64 us (3%)
  other arithmetic  0.61 us (3%)
    pallas_call x1, Pallas kernels, on_device(): pl.pallas_call(functools.partial(kernel, n_sec, n_grp), out_shape=[jax.Sh...  18.1 us
    add x1, other arithmetic, on_device(): return (half + 0.5 * timestep * speed, speed, accel)  0.61 us

profile of v1, /device:TPU:0, one launch (start us, length us, event | category | flops | bytes accessed | tf_op | source)
XLA Modules:
  0.0 19.3 jit_solution(13763560196909232444)
XLA Ops:
  0.6 18.1 %leapfrog.1 = (f32[3,512]{1,0:T(4,128)S(1)}, f32[3,512]{1,0:T(4,128)S(1)}, f32[3,512]{1,0:T(4,128)S(1)}, f32[3,512]{1,0:T(4,128)S(1)}) custom-call(f32[3,512]{1,0:T(4,128)} %pos_hbm.1, f32[3,512]{1,0:T(4,128)} %vel_hbm.1, f32[1,512]{1,0:T(1,128)} %bitcast.1, s32[2,64]{1,0:T(2,128)} %near_hbm.1, s32[2]{0:T(128)} %count_hbm.1, s32[2,32]{1,0:T(2,128)} %far_hbm.1), custom_call_target="tpu_custom_call" | custom-call | tf_op jit(solution)/shard_map/leapfrog/pallas_call | solution.py:303
  18.7 0.6 %multiply_add_fusion = (f32[3,512]{1,0:T(4,128)}, f32[3,512]{1,0:T(4,128)}, f32[3,512]{1,0:T(4,128)}) fusion(f32[3,512]{1,0:T(4,128)S(1)} %get-tuple-element.7, f32[3,512]{1,0:T(4,128)S(1)} %get-tuple-element.8, f32[3,512]{1,0:T(4,128)S(1)} %get-tuple-element.9, f32[3,512]{1,0:T(4,128)S(1)} %get-tuple-element.10), kind=kLoop, calls=%fused_computation | loop fusion | flops 7680 | bytes 43008 | tf_op jit(solution)/shard_map/add | solution.py:331

commit v2 on v1

--- a/solution.py
+++ b/solution.py
@@ -11,6 +11,15 @@
 softening = 0.25
 LANES = 128
 ROWS = 8
+PLACES = 16
+UNROLL = 64
+TARGET_ORDER = (0, 1, 2, 0, 1, 0, 2, 1)
+SOURCE_ORDER = (0, 0, 0, 1, 1, 2, 1, 2)
+
+
+def by_distance(n):
+    return sorted(range(n), key=lambda b: min(b, n - b))
+
 MESH = pl.DeviceIdType.MESH
 
 
@@ -21,13 +30,35 @@
     return pair * 2 + lax.rem(sec + r, 2)
 
 
+def each_other(n_sec, n_grp, sec, grp, act):
+    if n_sec * n_grp > UNROLL:
+
+        def one(r, carry):
+            other = lax.rem(sec * n_grp + grp + r, n_sec * n_grp)
+            act(other // n_grp, lax.rem(other, n_grp))
+            return carry
+
+        lax.fori_loop(1, n_sec * n_grp, one, 0)
+        return
+    secs = [sec] + [lax.rem(sec + a, n_sec) for a in range(1, n_sec)]
+    grps = [grp] + [lax.rem(grp + b, n_grp) for b in range(1, n_grp)]
+    for b in by_distance(n_grp):
+        for a in range(n_sec):
+            if a or b:
+                act(secs[a], grps[b])
+
+
 def own_moments(blocks):
+    width = LANES // len(blocks)
     lane = lax.broadcasted_iota(jnp.int32, (1, LANES), 1)
-    rows = []
-    for x, y, z, m in blocks:
+    place, inside = lane % PLACES, lane % width
+    row = jnp.zeros((1, LANES), jnp.float32)
+    middles = []
+    for b, (x, y, z, m) in enumerate(blocks):
         total = lambda v: jnp.sum(v, axis=1, keepdims=True)
         mass = total(m)
         cx, cy, cz = total(m * x) / mass, total(m * y) / mass, total(m * z) / mass
+        middles.append((cx, cy, cz))
         dx, dy, dz = x - cx, y - cy, z - cz
         radius = dx * dx + dy * dy + dz * dz
         numbers = (
@@ -42,11 +73,27 @@
             total(3.0 * m * dx * dz),
             total(3.0 * m * dy * dz),
         )
-        row = jnp.zeros((1, LANES), jnp.float32)
-        for place, number in enumerate(numbers):
-            row = jnp.where(lane == place, number, row)
-        rows.append(row)
-    return rows
+        own = jnp.zeros((1, LANES), jnp.float32)
+        for k, number in enumerate(numbers):
+            own = jnp.where(place == k, number, own)
+        row = jnp.where(lane // width == b, own, row)
+    high = row.astype(jnp.bfloat16).astype(jnp.float32)
+    rest = row - high
+    middle = rest.astype(jnp.bfloat16).astype(jnp.float32)
+    low = (rest - middle).astype(jnp.bfloat16).astype(jnp.float32)
+    row = jnp.where(inside < PLACES, high, jnp.where(inside < 2 * PLACES, middle, low))
+    return row, [sum(c) / len(blocks) for c in zip(*middles)]
+
+
+def three_parts(v):
+    high = v.astype(jnp.bfloat16).astype(jnp.float32)
+    rest = v - high
+    middle = rest.astype(jnp.bfloat16).astype(jnp.float32)
+    return high, middle, rest - middle
+
+
+def paired(parts, order):
+    return jnp.concatenate([parts[k] for k in order], axis=0).astype(jnp.bfloat16)
 
 
 def far_part(target, moment):
@@ -94,6 +141,7 @@
     ghosts,
     gathered,
     times,
+    chosen,
     send_sem,
     recv_sem,
     moment_send,
@@ -105,7 +153,6 @@
     particles = pos_ref.shape[1]
     block_size = particles // local_blocks
     group_blocks = n_sec * local_blocks
-    all_blocks = n_dev * local_blocks
     sec = lax.axis_index("sec")
     grp = lax.axis_index("grp")
     me = sec * n_grp + grp
@@ -127,17 +174,12 @@
         load.start()
     barrier = pltpu.get_barrier_semaphore()
 
-    def greet(r, carry):
-        other = lax.rem(me + r, n_dev)
+    def greet(to_sec, to_grp):
         pl.semaphore_signal(
-            barrier,
-            inc=1,
-            device_id={"sec": other // n_grp, "grp": lax.rem(other, n_grp)},
-            device_id_type=MESH,
-        )
-        return carry
-
-    lax.fori_loop(1, n_dev, greet, 0)
+            barrier, inc=1, device_id={"sec": to_sec, "grp": to_grp}, device_id_type=MESH
+        )
+
+    each_other(n_sec, n_grp, sec, grp, greet)
     for load in loads:
         load.wait()
 
@@ -151,11 +193,13 @@
             jnp.sum(used, axis=1, keepdims=True), (group_blocks, LANES)
         )
     entries = far_ref.shape[1]
-    block_number = lax.broadcasted_iota(jnp.int32, (all_blocks, entries), 0)
-    chosen = [
-        jnp.where(far_ref[b : b + 1, :] == block_number, 1.0, 0.0)
-        for b in range(local_blocks)
-    ]
+    for b in range(local_blocks):
+        picked = far_ref[b : b + 1, :]
+        for half_of in range(local_blocks):
+            number = lax.broadcasted_iota(jnp.int32, (n_dev, entries), 0) * local_blocks + half_of
+            chosen[b * entries : (b + 1) * entries, half_of * n_dev : (half_of + 1) * n_dev] = (
+                jnp.transpose(jnp.where(picked == number, 1.0, 0.0))
+            )
 
     current = pos_ref[...]
     speed = vel_ref[...]
@@ -165,10 +209,31 @@
         half = current + 0.5 * timestep * speed
         ghosts[step, sec, 0:3, :] = half
         ghosts[step, sec, 3:4, :] = mass_ref[...]
+
+        blocks = []
+        for b in range(local_blocks):
+            cut = slice(b * block_size, (b + 1) * block_size)
+            blocks.append(
+                (half[0:1, cut], half[1:2, cut], half[2:3, cut], mass_ref[0:1, cut])
+            )
+        gathered[step, me], origin = own_moments(blocks)
         if step == 0:
             pl.semaphore_wait(barrier, n_dev - 1)
-
-        def send_particles(r, carry):
+        mine = gathered.at[step, me]
+
+        def send_moments(to_sec, to_grp):
+            pltpu.make_async_remote_copy(
+                src_ref=mine,
+                dst_ref=mine,
+                send_sem=moment_send.at[step],
+                recv_sem=moment_recv.at[step],
+                device_id={"sec": to_sec, "grp": to_grp},
+                device_id_type=MESH,
+            ).start()
+
+        each_other(n_sec, n_grp, sec, grp, send_moments)
+
+        for r in range(1, n_sec):
             other = lax.rem(sec + r, n_sec)
             pltpu.make_async_remote_copy(
                 src_ref=ghosts.at[step, sec],
@@ -178,33 +243,24 @@
                 device_id={"sec": other, "grp": grp},
                 device_id_type=MESH,
             ).start()
-            return carry
-
-        lax.fori_loop(1, n_sec, send_particles, 0)
-
-        blocks = []
-        for b in range(local_blocks):
-            cut = slice(b * block_size, (b + 1) * block_size)
-            blocks.append(
-                (half[0:1, cut], half[1:2, cut], half[2:3, cut], mass_ref[0:1, cut])
-            )
-        for b, row in enumerate(own_moments(blocks)):
-            gathered[step, me * local_blocks + b] = row
-
-        def send_moments(r, carry):
-            other = lax.rem(me + r, n_dev)
-            mine = gathered.at[step, pl.ds(me * local_blocks, local_blocks)]
-            pltpu.make_async_remote_copy(
-                src_ref=mine,
-                dst_ref=mine,
-                send_sem=moment_send.at[step],
-                recv_sem=moment_recv.at[step],
-                device_id={"sec": other // n_grp, "grp": lax.rem(other, n_grp)},
-                device_id_type=MESH,
-            ).start()
-            return carry
-
-        lax.fori_loop(1, n_dev, send_moments, 0)
+
+        line = lax.broadcasted_iota(jnp.int32, (ROWS, 1), 0)
+        shift = jnp.where(
+            line == 0, origin[0], jnp.where(line == 1, origin[1], jnp.where(line == 2, origin[2], 0.0))
+        )
+        near = [half[c : c + 1, :] - origin[c] for c in range(3)]
+        reach = near[0] * near[0] + near[1] * near[1] + near[2] * near[2]
+        one = jnp.ones_like(reach)
+        target_side = paired(
+            three_parts(
+                jnp.concatenate(
+                    [-2.0 * near[0], -2.0 * near[1], -2.0 * near[2], one, reach]
+                    + [jnp.zeros_like(reach)] * 3,
+                    axis=0,
+                )
+            ),
+            TARGET_ORDER,
+        )
 
         def add_device(r, totals):
             other = peer(sec, r, n_sec)
@@ -218,6 +274,18 @@
             totals = [list(t) for t in totals]
             for tile in range(tiles):
                 rows = ghosts[step, other, :, tile * LANES : (tile + 1) * LANES]
+                rows = jnp.concatenate([rows, jnp.zeros_like(rows)], axis=0) - shift
+                moved = jnp.where(line < 3, rows, 0.0)
+                reach = jnp.sum(moved * moved, axis=0, keepdims=True) + softening
+                source_side = three_parts(
+                    jnp.where(line == 3, reach, jnp.where(line == 4, 1.0, moved))
+                )
+                square = lax.dot_general(
+                    paired(source_side, SOURCE_ORDER),
+                    target_side,
+                    (((0,), (0,)), ((), ())),
+                    preferred_element_type=jnp.float32,
+                )
                 columns = jnp.transpose(rows)
                 place = tile // tiles_of_block
                 weights = [
@@ -231,41 +299,45 @@
                     )
                     scaled = [sm * w for w in weights]
                     for t in range(tiles):
-                        lanes = slice(t * LANES, (t + 1) * LANES)
-                        dx = sx - half[0:1, lanes]
-                        dy = sy - half[1:2, lanes]
-                        dz = sz - half[2:3, lanes]
-                        inv = lax.rsqrt(dx * dx + dy * dy + (dz * dz + softening))
+                        inv = lax.rsqrt(square[cut, t * LANES : (t + 1) * LANES])
                         weight = scaled[t // tiles_of_block] * inv * (inv * inv)
-                        totals[t][0] = totals[t][0] + weight * dx
-                        totals[t][1] = totals[t][1] + weight * dy
-                        totals[t][2] = totals[t][2] + weight * dz
+                        totals[t][0] = totals[t][0] + weight * sx
+                        totals[t][1] = totals[t][1] + weight * sy
+                        totals[t][2] = totals[t][2] + weight * sz
+                        totals[t][3] = totals[t][3] + weight
             return tuple(tuple(t) for t in totals)
 
         zero = jnp.zeros((ROWS, LANES), jnp.float32)
-        totals = lax.fori_loop(0, n_sec, add_device, tuple((zero,) * 3 for _ in range(tiles)))
-        direct = jnp.concatenate(
-            [
-                jnp.concatenate(
-                    [jnp.sum(totals[t][c], axis=0, keepdims=True) for t in range(tiles)], axis=1
-                )
-                for c in range(3)
-            ],
+        totals = lax.fori_loop(0, n_sec, add_device, tuple((zero,) * 4 for _ in range(tiles)))
+        summed = [
+            jnp.concatenate(
+                [jnp.sum(totals[t][c], axis=0, keepdims=True) for t in range(tiles)], axis=1
+            )
+            for c in range(4)
+        ]
+        direct = jnp.concatenate([summed[c] - near[c] * summed[3] for c in range(3)], axis=0)
+
+        others = gathered.at[step, pl.ds(0, n_dev - 1)]
+        pltpu.make_async_copy(others, others, moment_recv.at[step]).wait()
+        table = gathered[step].reshape(n_dev, LANES)
+        width = LANES // local_blocks
+        table = jnp.concatenate(
+            [pltpu.roll(table, LANES - b * width, 1) if b else table for b in range(local_blocks)],
             axis=0,
         )
-
-        others = gathered.at[step, pl.ds(0, (n_dev - 1) * local_blocks)]
-        pltpu.make_async_copy(others, others, moment_recv.at[step]).wait()
-        table = gathered[step].reshape(all_blocks, LANES)
+        parts = jnp.dot(
+            chosen[...].astype(jnp.bfloat16),
+            table.astype(jnp.bfloat16),
+            preferred_element_type=jnp.float32,
+        )
+        parts = (
+            parts
+            + pltpu.roll(parts, LANES - PLACES, 1)
+            + pltpu.roll(parts, LANES - 2 * PLACES, 1)
+        )
         far = []
         for b in range(local_blocks):
-            moment = lax.dot_general(
-                chosen[b],
-                table,
-                (((0,), (0,)), ((), ())),
-                precision=lax.Precision.HIGHEST,
-                preferred_element_type=jnp.float32,
-            )
+            moment = parts[b * entries : (b + 1) * entries]
             cut = slice(b * block_size, (b + 1) * block_size)
             far.append(
                 jnp.concatenate(
@@ -292,7 +364,7 @@
             return carry
 
         lax.fori_loop(1, n_sec, sent, 0)
-        others = gathered.at[step, pl.ds(0, (n_dev - 1) * local_blocks)]
+        others = gathered.at[step, pl.ds(0, n_dev - 1)]
         pltpu.make_async_copy(others, others, moment_send.at[step]).wait()
 
 
@@ -314,8 +386,11 @@
             pltpu.VMEM(far_list.shape, jnp.int32),
             pltpu.SemaphoreType.DMA((6,)),
             pltpu.VMEM((2, n_sec, 4, particles), jnp.float32),
-            pltpu.VMEM((2, n_sec * n_grp * local_blocks, 1, LANES), jnp.float32),
+            pltpu.VMEM((2, n_sec * n_grp, 1, LANES), jnp.float32),
             pltpu.VMEM((local_blocks, n_sec * local_blocks, LANES), jnp.float32),
+            pltpu.VMEM(
+                (local_blocks * far_list.shape[1], n_sec * n_grp * local_blocks), jnp.float32
+            ),
             pltpu.SemaphoreType.DMA((2, n_sec)),
             pltpu.SemaphoreType.DMA((2, n_sec)),
             pltpu.SemaphoreType.DMA((2,)),

time: 19.5 us -> 18.8 us (0.964)
  Pallas kernels: 18.1 us -> 17.4 us
    pallas_call x1, Pallas kernels: 18.1 us -> 17.4 us  [on_device(): pl.pallas_call(functools.partial(kernel, n_sec, n_grp), out_shape=[jax.Sh...]
where the time goes in v2:
time: 18.8 us; the launch traced here: 18.6 us
  Pallas kernels  17.4 us (93%)
  between operations  0.64 us (3%)
  other arithmetic  0.61 us (3%)
    pallas_call x1, Pallas kernels, on_device(): pl.pallas_call(functools.partial(kernel, n_sec, n_grp), out_shape=[jax.Sh...  17.4 us
    add x1, other arithmetic, on_device(): return (half + 0.5 * timestep * speed, speed, accel)  0.61 us

profile of v2, /device:TPU:0, one launch (start us, length us, event | category | flops | bytes accessed | tf_op | source)
XLA Modules:
  0.0 18.6 jit_solution(9937254379606608024)
XLA Ops:
  0.6 17.4 %leapfrog.1 = (f32[3,512]{1,0:T(4,128)S(1)}, f32[3,512]{1,0:T(4,128)S(1)}, f32[3,512]{1,0:T(4,128)S(1)}, f32[3,512]{1,0:T(4,128)S(1)}) custom-call(f32[3,512]{1,0:T(4,128)} %pos_hbm.1, f32[3,512]{1,0:T(4,128)} %vel_hbm.1, f32[1,512]{1,0:T(1,128)} %bitcast.1, s32[2,64]{1,0:T(2,128)} %near_hbm.1, s32[2]{0:T(128)} %count_hbm.1, s32[2,32]{1,0:T(2,128)} %far_hbm.1), custom_call_target="tpu_custom_call" | custom-call | tf_op jit(solution)/shard_map/leapfrog/pallas_call | solution.py:375
  18.0 0.6 %multiply_add_fusion = (f32[3,512]{1,0:T(4,128)}, f32[3,512]{1,0:T(4,128)}, f32[3,512]{1,0:T(4,128)}) fusion(f32[3,512]{1,0:T(4,128)S(1)} %get-tuple-element.7, f32[3,512]{1,0:T(4,128)S(1)} %get-tuple-element.8, f32[3,512]{1,0:T(4,128)S(1)} %get-tuple-element.9, f32[3,512]{1,0:T(4,128)S(1)} %get-tuple-element.10), kind=kLoop, calls=%fused_computation | loop fusion | flops 7680 | bytes 43008 | tf_op jit(solution)/shard_map/add | solution.py:406

commit v3 on v2

--- a/solution.py
+++ b/solution.py
@@ -11,6 +11,7 @@
 softening = 0.25
 LANES = 128
 ROWS = 8
+NUMBERS = 10
 PLACES = 16
 UNROLL = 64
 TARGET_ORDER = (0, 1, 2, 0, 1, 0, 2, 1)
@@ -18,7 +19,7 @@
 
 
 def by_distance(n):
-    return sorted(range(n), key=lambda b: min(b, n - b))
+    return sorted(range(n), key=lambda b: min(b, n - b) if b else 1.5)
 
 MESH = pl.DeviceIdType.MESH
 
@@ -48,7 +49,7 @@
                 act(secs[a], grps[b])
 
 
-def own_moments(blocks):
+def own_moments(blocks, about):
     width = LANES // len(blocks)
     lane = lax.broadcasted_iota(jnp.int32, (1, LANES), 1)
     place, inside = lane % PLACES, lane % width
@@ -57,21 +58,28 @@
     for b, (x, y, z, m) in enumerate(blocks):
         total = lambda v: jnp.sum(v, axis=1, keepdims=True)
         mass = total(m)
-        cx, cy, cz = total(m * x) / mass, total(m * y) / mass, total(m * z) / mass
-        middles.append((cx, cy, cz))
-        dx, dy, dz = x - cx, y - cy, z - cz
-        radius = dx * dx + dy * dy + dz * dz
+        if about is None:
+            px, py, pz = total(m * x) / mass, total(m * y) / mass, total(m * z) / mass
+        else:
+            px, py, pz = about[b]
+        dx, dy, dz = x - px, y - py, z - pz
+        mx, my, mz = m * dx, m * dy, m * dz
+        sx, sy, sz = total(mx), total(my), total(mz)
+        xx, yy, zz = total(mx * dx), total(my * dy), total(mz * dz)
+        xy, xz, yz = total(mx * dy), total(mx * dz), total(my * dz)
+        ox, oy, oz = sx / mass, sy / mass, sz / mass
+        xx, yy, zz = xx - sx * ox, yy - sy * oy, zz - sz * oz
+        xy, xz, yz = xy - sx * oy, xz - sx * oz, yz - sy * oz
+        middles.append((px + ox, py + oy, pz + oz))
         numbers = (
             mass,
-            cx,
-            cy,
-            cz,
-            total(m * (3.0 * dx * dx - radius)),
-            total(m * (3.0 * dy * dy - radius)),
-            total(m * (3.0 * dz * dz - radius)),
-            total(3.0 * m * dx * dy),
-            total(3.0 * m * dx * dz),
-            total(3.0 * m * dy * dz),
+            *middles[-1],
+            2.0 * xx - yy - zz,
+            2.0 * yy - xx - zz,
+            2.0 * zz - xx - yy,
+            3.0 * xy,
+            3.0 * xz,
+            3.0 * yz,
         )
         own = jnp.zeros((1, LANES), jnp.float32)
         for k, number in enumerate(numbers):
@@ -82,7 +90,7 @@
     middle = rest.astype(jnp.bfloat16).astype(jnp.float32)
     low = (rest - middle).astype(jnp.bfloat16).astype(jnp.float32)
     row = jnp.where(inside < PLACES, high, jnp.where(inside < 2 * PLACES, middle, low))
-    return row, [sum(c) / len(blocks) for c in zip(*middles)]
+    return row, middles
 
 
 def three_parts(v):
@@ -97,24 +105,22 @@
 
 
 def far_part(target, moment):
-    number = [moment[:, k : k + 1] for k in range(10)]
-    mass, cx, cy, cz, qxx, qyy, qzz, qxy, qxz, qyz = number
+    mass, cx, cy, cz, qxx, qyy, qzz, qxy, qxz, qyz = moment
     rx, ry, rz = target[0] - cx, target[1] - cy, target[2] - cz
     square = rx * rx + ry * ry + rz * rz + softening
     inv = lax.rsqrt(square)
     inv_two = inv * inv
-    inv_three = inv_two * inv
-    inv_five = inv_three * inv_two
+    inv_five = inv_two * inv_two * inv
     quad_x = qxx * rx + qxy * ry + qxz * rz
     quad_y = qxy * rx + qyy * ry + qyz * rz
     quad_z = qxz * rx + qyz * ry + qzz * rz
     inner = rx * quad_x + ry * quad_y + rz * quad_z
-    radial = 2.5 * inner * inv_two * inv_five - mass * inv_three
+    radial = 2.5 * inner * inv_two - mass * square
     total = lambda v: jnp.sum(v, axis=0, keepdims=True)
     return (
-        total(radial * rx - quad_x * inv_five),
-        total(radial * ry - quad_y * inv_five),
-        total(radial * rz - quad_z * inv_five),
+        total((radial * rx - quad_x) * inv_five),
+        total((radial * ry - quad_y) * inv_five),
+        total((radial * rz - quad_z) * inv_five),
     )
 
 
@@ -142,6 +148,8 @@
     gathered,
     times,
     chosen,
+    spread,
+    target_side,
     send_sem,
     recv_sem,
     moment_send,
@@ -201,8 +209,14 @@
                 jnp.transpose(jnp.where(picked == number, 1.0, 0.0))
             )
 
+    middles = None
     current = pos_ref[...]
     speed = vel_ref[...]
+    source_lane = lax.broadcasted_iota(jnp.int32, (LANES, LANES), 0)
+    for k in range(NUMBERS):
+        spread[:, k * LANES : (k + 1) * LANES] = jnp.where(
+            (source_lane % PLACES == k) & (source_lane < 3 * PLACES), 1.0, 0.0
+        ).astype(jnp.bfloat16)
     tiles = particles // LANES
     tiles_of_block = block_size // LANES
     for step in range(2):
@@ -216,7 +230,8 @@
             blocks.append(
                 (half[0:1, cut], half[1:2, cut], half[2:3, cut], mass_ref[0:1, cut])
             )
-        gathered[step, me], origin = own_moments(blocks)
+        gathered[step, me], middles = own_moments(blocks, middles)
+        origin = [sum(c) / local_blocks for c in zip(*middles)]
         if step == 0:
             pl.semaphore_wait(barrier, n_dev - 1)
         mine = gathered.at[step, me]
@@ -248,19 +263,21 @@
         shift = jnp.where(
             line == 0, origin[0], jnp.where(line == 1, origin[1], jnp.where(line == 2, origin[2], 0.0))
         )
-        near = [half[c : c + 1, :] - origin[c] for c in range(3)]
-        reach = near[0] * near[0] + near[1] * near[1] + near[2] * near[2]
-        one = jnp.ones_like(reach)
-        target_side = paired(
-            three_parts(
-                jnp.concatenate(
-                    [-2.0 * near[0], -2.0 * near[1], -2.0 * near[2], one, reach]
-                    + [jnp.zeros_like(reach)] * 3,
-                    axis=0,
-                )
-            ),
-            TARGET_ORDER,
-        )
+
+        @pl.when(sec >= 0)
+        def _():
+            near = [half[c : c + 1, :] - origin[c] for c in range(3)]
+            reach = near[0] * near[0] + near[1] * near[1] + near[2] * near[2]
+            target_side[...] = paired(
+                three_parts(
+                    jnp.concatenate(
+                        [-2.0 * near[0], -2.0 * near[1], -2.0 * near[2], jnp.ones_like(reach), reach]
+                        + [jnp.zeros_like(reach)] * 3,
+                        axis=0,
+                    )
+                ),
+                TARGET_ORDER,
+            )
 
         def add_device(r, totals):
             other = peer(sec, r, n_sec)
@@ -282,7 +299,7 @@
                 )
                 square = lax.dot_general(
                     paired(source_side, SOURCE_ORDER),
-                    target_side,
+                    target_side[...],
                     (((0,), (0,)), ((), ())),
                     preferred_element_type=jnp.float32,
                 )
@@ -315,9 +332,16 @@
             )
             for c in range(4)
         ]
-        direct = jnp.concatenate([summed[c] - near[c] * summed[3] for c in range(3)], axis=0)
+        direct = jnp.concatenate(
+            [summed[c] - (half[c : c + 1, :] - origin[c]) * summed[3] for c in range(3)], axis=0
+        )
 
         others = gathered.at[step, pl.ds(0, n_dev - 1)]
+        for r in range(1, n_sec):
+            pltpu.make_async_copy(
+                ghosts.at[step, sec], ghosts.at[step, sec], send_sem.at[step, lax.rem(sec + r, n_sec)]
+            ).wait()
+        pltpu.make_async_copy(others, others, moment_send.at[step]).wait()
         pltpu.make_async_copy(others, others, moment_recv.at[step]).wait()
         table = gathered[step].reshape(n_dev, LANES)
         width = LANES // local_blocks
@@ -330,14 +354,19 @@
             table.astype(jnp.bfloat16),
             preferred_element_type=jnp.float32,
         )
-        parts = (
-            parts
-            + pltpu.roll(parts, LANES - PLACES, 1)
-            + pltpu.roll(parts, LANES - 2 * PLACES, 1)
+        numbers = jnp.dot(
+            parts.astype(jnp.bfloat16), spread[...], preferred_element_type=jnp.float32
         )
         far = []
         for b in range(local_blocks):
-            moment = parts[b * entries : (b + 1) * entries]
+            moment = [
+                jnp.concatenate(
+                    [numbers[b * entries : (b + 1) * entries, k * LANES : (k + 1) * LANES]]
+                    * tiles_of_block,
+                    axis=1,
+                )
+                for k in range(NUMBERS)
+            ]
             cut = slice(b * block_size, (b + 1) * block_size)
             far.append(
                 jnp.concatenate(
@@ -353,19 +382,6 @@
             half_out[...] = half
             direct_out[...] = direct
             far_out[...] = far
-
-    for step in range(2):
-
-        def sent(r, carry):
-            other = lax.rem(sec + r, n_sec)
-            pltpu.make_async_copy(
-                ghosts.at[step, sec], ghosts.at[step, sec], send_sem.at[step, other]
-            ).wait()
-            return carry
-
-        lax.fori_loop(1, n_sec, sent, 0)
-        others = gathered.at[step, pl.ds(0, n_dev - 1)]
-        pltpu.make_async_copy(others, others, moment_send.at[step]).wait()
 
 
 def on_device(n_sec, n_grp, positions, velocities, masses, near_list, near_count, far_list):
@@ -391,6 +407,8 @@
             pltpu.VMEM(
                 (local_blocks * far_list.shape[1], n_sec * n_grp * local_blocks), jnp.float32
             ),
+            pltpu.VMEM((LANES, NUMBERS * LANES), jnp.bfloat16),
+            pltpu.VMEM((len(TARGET_ORDER) * ROWS, particles), jnp.bfloat16),
             pltpu.SemaphoreType.DMA((2, n_sec)),
             pltpu.SemaphoreType.DMA((2, n_sec)),
             pltpu.SemaphoreType.DMA((2,)),

time: 18.8 us -> 18.5 us (0.984)
  Pallas kernels: 17.4 us -> 17 us
    pallas_call x1, Pallas kernels: 17.4 us -> 17 us  [on_device(): pl.pallas_call(functools.partial(kernel, n_sec, n_grp), out_shape=[jax.Sh...]
where the time goes in v3:
time: 18.5 us; the launch traced here: 18.3 us
  Pallas kernels  17 us (92%)
  between operations  0.64 us (3%)
  other arithmetic  0.61 us (3%)
    pallas_call x1, Pallas kernels, on_device(): pl.pallas_call(functools.partial(kernel, n_sec, n_grp), out_shape=[jax.Sh...  17 us
    add x1, other arithmetic, on_device(): return (half + 0.5 * timestep * speed, speed, accel)  0.61 us

profile of v3, /device:TPU:0, one launch (start us, length us, event | category | flops | bytes accessed | tf_op | source)
XLA Modules:
  0.0 18.3 jit_solution(1605274698844885402)
XLA Ops:
  0.6 17.0 %leapfrog.1 = (f32[3,512]{1,0:T(4,128)S(1)}, f32[3,512]{1,0:T(4,128)S(1)}, f32[3,512]{1,0:T(4,128)S(1)}, f32[3,512]{1,0:T(4,128)S(1)}) custom-call(f32[3,512]{1,0:T(4,128)} %pos_hbm.1, f32[3,512]{1,0:T(4,128)} %vel_hbm.1, f32[1,512]{1,0:T(1,128)} %bitcast.1, s32[2,64]{1,0:T(2,128)} %near_hbm.1, s32[2]{0:T(128)} %count_hbm.1, s32[2,32]{1,0:T(2,128)} %far_hbm.1), custom_call_target="tpu_custom_call" | custom-call | tf_op jit(solution)/shard_map/leapfrog/pallas_call | solution.py:391
  17.7 0.6 %multiply_add_fusion = (f32[3,512]{1,0:T(4,128)}, f32[3,512]{1,0:T(4,128)}, f32[3,512]{1,0:T(4,128)}) fusion(f32[3,512]{1,0:T(4,128)S(1)} %get-tuple-element.7, f32[3,512]{1,0:T(4,128)S(1)} %get-tuple-element.8, f32[3,512]{1,0:T(4,128)S(1)} %get-tuple-element.9, f32[3,512]{1,0:T(4,128)S(1)} %get-tuple-element.10), kind=kLoop, calls=%fused_computation | loop fusion | flops 7680 | bytes 43008 | tf_op jit(solution)/shard_map/add | solution.py:424

commit v4 on v3

--- a/solution.py
+++ b/solution.py
@@ -143,16 +143,15 @@
     near_ref,
     count_ref,
     far_ref,
-    load_sem,
     ghosts,
     gathered,
     times,
     chosen,
+    kept,
     spread,
     target_side,
     send_sem,
     recv_sem,
-    moment_send,
     moment_recv,
 ):
     n_dev = n_sec * n_grp
@@ -165,31 +164,35 @@
     grp = lax.axis_index("grp")
     me = sec * n_grp + grp
 
-    loads = [
-        pltpu.make_async_copy(source, target, load_sem.at[k])
-        for k, (source, target) in enumerate(
-            (
-                (pos_hbm, pos_ref),
-                (vel_hbm, vel_ref),
-                (mass_hbm, mass_ref),
-                (near_hbm, near_ref),
-                (count_hbm, count_ref),
-                (far_hbm, far_ref),
-            )
-        )
-    ]
-    for load in loads:
-        load.start()
     barrier = pltpu.get_barrier_semaphore()
 
-    def greet(to_sec, to_grp):
-        pl.semaphore_signal(
-            barrier, inc=1, device_id={"sec": to_sec, "grp": to_grp}, device_id_type=MESH
-        )
-
-    each_other(n_sec, n_grp, sec, grp, greet)
-    for load in loads:
-        load.wait()
+    def take(load_sem):
+        loads = [
+            pltpu.make_async_copy(source, target, load_sem.at[k])
+            for k, (source, target) in enumerate(
+                (
+                    (pos_hbm, pos_ref),
+                    (vel_hbm, vel_ref),
+                    (mass_hbm, mass_ref),
+                    (near_hbm, near_ref),
+                    (count_hbm, count_ref),
+                    (far_hbm, far_ref),
+                )
+            )
+        ]
+        for load in loads:
+            load.start()
+
+        def greet(to_sec, to_grp):
+            pl.semaphore_signal(
+                barrier, inc=1, device_id={"sec": to_sec, "grp": to_grp}, device_id_type=MESH
+            )
+
+        each_other(n_sec, n_grp, sec, grp, greet)
+        for load in loads:
+            load.wait()
+
+    pl.run_scoped(take, pltpu.SemaphoreType.DMA((6,)))
 
     number = lax.broadcasted_iota(jnp.int32, (group_blocks, slots), 0)
     slot = lax.broadcasted_iota(jnp.int32, (group_blocks, slots), 1)
@@ -201,21 +204,26 @@
             jnp.sum(used, axis=1, keepdims=True), (group_blocks, LANES)
         )
     entries = far_ref.shape[1]
+    width = LANES // local_blocks
+    half_of_lane = lax.broadcasted_iota(jnp.int32, (entries, LANES), 1) // width
+    number = lax.broadcasted_iota(jnp.int32, (n_dev, entries), 0)
     for b in range(local_blocks):
+        rows = slice(b * entries, (b + 1) * entries)
         picked = far_ref[b : b + 1, :]
-        for half_of in range(local_blocks):
-            number = lax.broadcasted_iota(jnp.int32, (n_dev, entries), 0) * local_blocks + half_of
-            chosen[b * entries : (b + 1) * entries, half_of * n_dev : (half_of + 1) * n_dev] = (
-                jnp.transpose(jnp.where(picked == number, 1.0, 0.0))
-            )
+        chosen[rows, :] = jnp.transpose(jnp.where(picked // local_blocks == number, 1.0, 0.0))
+        place = jnp.transpose(
+            jnp.broadcast_to((picked % local_blocks).astype(jnp.float32), (LANES, entries))
+        )
+        kept[rows, :] = jnp.where(place == half_of_lane.astype(jnp.float32), 1.0, 0.0)
 
     middles = None
     current = pos_ref[...]
     speed = vel_ref[...]
+
     source_lane = lax.broadcasted_iota(jnp.int32, (LANES, LANES), 0)
     for k in range(NUMBERS):
         spread[:, k * LANES : (k + 1) * LANES] = jnp.where(
-            (source_lane % PLACES == k) & (source_lane < 3 * PLACES), 1.0, 0.0
+            (source_lane % PLACES == k) & (source_lane % width < 3 * PLACES), 1.0, 0.0
         ).astype(jnp.bfloat16)
     tiles = particles // LANES
     tiles_of_block = block_size // LANES
@@ -240,7 +248,7 @@
             pltpu.make_async_remote_copy(
                 src_ref=mine,
                 dst_ref=mine,
-                send_sem=moment_send.at[step],
+                send_sem=send_sem.at[1],
                 recv_sem=moment_recv.at[step],
                 device_id={"sec": to_sec, "grp": to_grp},
                 device_id_type=MESH,
@@ -253,8 +261,8 @@
             pltpu.make_async_remote_copy(
                 src_ref=ghosts.at[step, sec],
                 dst_ref=ghosts.at[step, sec],
-                send_sem=send_sem.at[step, other],
-                recv_sem=recv_sem.at[step, sec],
+                send_sem=send_sem.at[0],
+                recv_sem=recv_sem.at[step, r - 1],
                 device_id={"sec": other, "grp": grp},
                 device_id_type=MESH,
             ).start()
@@ -285,7 +293,9 @@
             @pl.when(r > 0)
             def _():
                 pltpu.make_async_copy(
-                    ghosts.at[step, other], ghosts.at[step, other], recv_sem.at[step, other]
+                    ghosts.at[step, other],
+                    ghosts.at[step, other],
+                    recv_sem.at[step, lax.rem(sec - other + n_sec, n_sec) - 1],
                 ).wait()
 
             totals = [list(t) for t in totals]
@@ -337,25 +347,18 @@
         )
 
         others = gathered.at[step, pl.ds(0, n_dev - 1)]
-        for r in range(1, n_sec):
-            pltpu.make_async_copy(
-                ghosts.at[step, sec], ghosts.at[step, sec], send_sem.at[step, lax.rem(sec + r, n_sec)]
-            ).wait()
-        pltpu.make_async_copy(others, others, moment_send.at[step]).wait()
+        sent = ghosts.at[step, pl.ds(0, n_sec - 1)]
+        pltpu.make_async_copy(sent, sent, send_sem.at[0]).wait()
+        pltpu.make_async_copy(others, others, send_sem.at[1]).wait()
         pltpu.make_async_copy(others, others, moment_recv.at[step]).wait()
         table = gathered[step].reshape(n_dev, LANES)
-        width = LANES // local_blocks
-        table = jnp.concatenate(
-            [pltpu.roll(table, LANES - b * width, 1) if b else table for b in range(local_blocks)],
-            axis=0,
-        )
         parts = jnp.dot(
             chosen[...].astype(jnp.bfloat16),
             table.astype(jnp.bfloat16),
             preferred_element_type=jnp.float32,
         )
         numbers = jnp.dot(
-            parts.astype(jnp.bfloat16), spread[...], preferred_element_type=jnp.float32
+            (parts * kept[...]).astype(jnp.bfloat16), spread[...], preferred_element_type=jnp.float32
         )
         far = []
         for b in range(local_blocks):
@@ -400,18 +403,17 @@
             pltpu.VMEM(near_list.shape, jnp.int32),
             pltpu.SMEM(near_count.shape, jnp.int32),
             pltpu.VMEM(far_list.shape, jnp.int32),
-            pltpu.SemaphoreType.DMA((6,)),
             pltpu.VMEM((2, n_sec, 4, particles), jnp.float32),
             pltpu.VMEM((2, n_sec * n_grp, 1, LANES), jnp.float32),
             pltpu.VMEM((local_blocks, n_sec * local_blocks, LANES), jnp.float32),
             pltpu.VMEM(
-                (local_blocks * far_list.shape[1], n_sec * n_grp * local_blocks), jnp.float32
+                (local_blocks * far_list.shape[1], n_sec * n_grp), jnp.float32
             ),
+            pltpu.VMEM((local_blocks * far_list.shape[1], LANES), jnp.float32),
             pltpu.VMEM((LANES, NUMBERS * LANES), jnp.bfloat16),
             pltpu.VMEM((len(TARGET_ORDER) * ROWS, particles), jnp.bfloat16),
-            pltpu.SemaphoreType.DMA((2, n_sec)),
-            pltpu.SemaphoreType.DMA((2, n_sec)),
             pltpu.SemaphoreType.DMA((2,)),
+            pltpu.SemaphoreType.DMA((2, n_sec - 1)),
             pltpu.SemaphoreType.DMA((2,)),
         ],
         compiler_params=pltpu.CompilerParams(

time: 18.5 us -> 18.2 us (0.984)
  Pallas kernels: 17 us -> 16.8 us
    pallas_call x1, Pallas kernels: 17 us -> 16.8 us  [on_device(): pl.pallas_call(functools.partial(kernel, n_sec, n_grp), out_shape=[jax.Sh...]
where the time goes in v4:
time: 18.2 us; the launch traced here: 18 us
  Pallas kernels  16.8 us (92%)
  between operations  0.64 us (4%)
  other arithmetic  0.61 us (3%)
    pallas_call x1, Pallas kernels, on_device(): pl.pallas_call(functools.partial(kernel, n_sec, n_grp), out_shape=[jax.Sh...  16.8 us
    add x1, other arithmetic, on_device(): return (half + 0.5 * timestep * speed, speed, accel)  0.61 us

profile of v4, /device:TPU:0, one launch (start us, length us, event | category | flops | bytes accessed | tf_op | source)
XLA Modules:
  0.0 18.0 jit_solution(16108473126279026256)
XLA Ops:
  0.6 16.8 %leapfrog.1 = (f32[3,512]{1,0:T(4,128)S(1)}, f32[3,512]{1,0:T(4,128)S(1)}, f32[3,512]{1,0:T(4,128)S(1)}, f32[3,512]{1,0:T(4,128)S(1)}) custom-call(f32[3,512]{1,0:T(4,128)} %pos_hbm.1, f32[3,512]{1,0:T(4,128)} %vel_hbm.1, f32[1,512]{1,0:T(1,128)} %bitcast.1, s32[2,64]{1,0:T(2,128)} %near_hbm.1, s32[2]{0:T(128)} %count_hbm.1, s32[2,32]{1,0:T(2,128)} %far_hbm.1), custom_call_target="tpu_custom_call" | custom-call | tf_op jit(solution)/shard_map/leapfrog/pallas_call | solution.py:394
  17.4 0.6 %multiply_add_fusion = (f32[3,512]{1,0:T(4,128)}, f32[3,512]{1,0:T(4,128)}, f32[3,512]{1,0:T(4,128)}) fusion(f32[3,512]{1,0:T(4,128)S(1)} %get-tuple-element.7, f32[3,512]{1,0:T(4,128)S(1)} %get-tuple-element.8, f32[3,512]{1,0:T(4,128)S(1)} %get-tuple-element.9, f32[3,512]{1,0:T(4,128)S(1)} %get-tuple-element.10), kind=kLoop, calls=%fused_computation | loop fusion | flops 7680 | bytes 43008 | tf_op jit(solution)/shard_map/add | solution.py:426

commit v5 on v4

--- a/solution.py
+++ b/solution.py
@@ -19,7 +19,7 @@
 
 
 def by_distance(n):
-    return sorted(range(n), key=lambda b: min(b, n - b) if b else 1.5)
+    return sorted(range(n), key=lambda b: min(b, n - b) if b else 2.5)
 
 MESH = pl.DeviceIdType.MESH
 
@@ -44,7 +44,7 @@
     secs = [sec] + [lax.rem(sec + a, n_sec) for a in range(1, n_sec)]
     grps = [grp] + [lax.rem(grp + b, n_grp) for b in range(1, n_grp)]
     for b in by_distance(n_grp):
-        for a in range(n_sec):
+        for a in range(n_sec - 1, -1, -1):
             if a or b:
                 act(secs[a], grps[b])
 
@@ -136,7 +136,6 @@
     half_out,
     vel_out,
     direct_out,
-    far_out,
     pos_ref,
     vel_ref,
     mass_ref,
@@ -383,19 +382,18 @@
             vel_out[...] = speed
         else:
             half_out[...] = half
-            direct_out[...] = direct
-            far_out[...] = far
+            direct_out[...] = 0.5 * (direct + far)
 
 
 def on_device(n_sec, n_grp, positions, velocities, masses, near_list, near_count, far_list):
     particles = positions.shape[1]
     local_blocks = near_list.shape[0]
     vmem = pl.BlockSpec(memory_space=pltpu.VMEM)
-    half, speed, direct, far = pl.pallas_call(
+    half, speed, halved = pl.pallas_call(
         functools.partial(kernel, n_sec, n_grp),
-        out_shape=[jax.ShapeDtypeStruct(positions.shape, jnp.float32)] * 4,
+        out_shape=[jax.ShapeDtypeStruct(positions.shape, jnp.float32)] * 3,
         in_specs=[pl.BlockSpec(memory_space=pltpu.HBM)] * 6,
-        out_specs=[vmem] * 4,
+        out_specs=[vmem] * 3,
         scratch_shapes=[
             pltpu.VMEM(positions.shape, jnp.float32),
             pltpu.VMEM(velocities.shape, jnp.float32),
@@ -421,7 +419,7 @@
         ),
         name="leapfrog",
     )(*[pltpu.with_memory_space_constraint(v, pltpu.HBM) for v in (positions, velocities, masses[None, :], near_list, near_count, far_list)])
-    accel = direct + far
+    accel = halved + halved
     speed = speed + timestep * accel
     return half + 0.5 * timestep * speed, speed, accel
 

time: 18.2 us -> 18.2 us (level)
  no operation moved by 1% of the time
where the time goes in v5:
time: 18.2 us; the launch traced here: 18 us
  Pallas kernels  16.8 us (92%)
  between operations  0.64 us (4%)
  other arithmetic  0.61 us (3%)
    pallas_call x1, Pallas kernels, on_device(): pl.pallas_call(functools.partial(kernel, n_sec, n_grp), out_shape=[jax.Sh...  16.8 us
    add x1, other arithmetic, on_device(): return (half + 0.5 * timestep * speed, speed, accel)  0.61 us

profile of v5, /device:TPU:0, one launch (start us, length us, event | category | flops | bytes accessed | tf_op | source)
XLA Modules:
  0.0 18.0 jit_solution(13019015997837458204)
XLA Ops:
  0.6 16.8 %leapfrog.1 = (f32[3,512]{1,0:T(4,128)S(1)}, f32[3,512]{1,0:T(4,128)S(1)}, f32[3,512]{1,0:T(4,128)S(1)}) custom-call(f32[3,512]{1,0:T(4,128)} %pos_hbm.1, f32[3,512]{1,0:T(4,128)} %vel_hbm.1, f32[1,512]{1,0:T(1,128)} %bitcast.1, s32[2,64]{1,0:T(2,128)} %near_hbm.1, s32[2]{0:T(128)} %count_hbm.1, s32[2,32]{1,0:T(2,128)} %far_hbm.1), custom_call_target="tpu_custom_call" | custom-call | tf_op jit(solution)/shard_map/leapfrog/pallas_call | solution.py:392
  17.4 0.6 %multiply_add_fusion = (f32[3,512]{1,0:T(4,128)}, f32[3,512]{1,0:T(4,128)}, f32[3,512]{1,0:T(4,128)}) fusion(f32[3,512]{1,0:T(4,128)S(1)} %get-tuple-element.6, f32[3,512]{1,0:T(4,128)S(1)} %get-tuple-element.7, f32[3,512]{1,0:T(4,128)S(1)} %get-tuple-element.8), kind=kLoop, calls=%fused_computation | loop fusion | flops 7680 | bytes 36864 | tf_op jit(solution)/shard_map/add | solution.py:424
